TPU v7x, 32 devices: a whole 2x2x4 slice. The times are simulated.
32 devices in a mesh: shard: 8 (over z, x), width: 4 (over y, core).
Axes of the slice: x: 2, y: 2, z: 4, core: 2. Of those that a mesh axis runs over, the one named last changes fastest.
Arguments:
- w_query: float32 [4096, 4096], P('shard', 'width'), may hold values from -0.125 to 0.125
- first_query: float32 [4096, 4096], P('shard', 'width'), may hold values from -0.09375 to 0.09375
- second_query: float32 [4096, 4096], P('shard', 'width'), may hold values from -0.09375 to 0.09375
- w_key: float32 [4096, 1024], P('shard', 'width'), may hold values from -0.125 to 0.125
- first_key: float32 [4096, 1024], P('shard', 'width'), may hold values from -0.09375 to 0.09375
- second_key: float32 [4096, 1024], P('shard', 'width'), may hold values from -0.09375 to 0.09375
- w_value: float32 [4096, 1024], P('shard', 'width'), may hold values from -0.125 to 0.125
- first_value: float32 [4096, 1024], P('shard', 'width'), may hold values from -0.09375 to 0.09375
- second_value: float32 [4096, 1024], P('shard', 'width'), may hold values from -0.09375 to 0.09375
- norm_train: float32 [4096], P(('shard', 'width')), may hold values from 0.25 to 1.75
- norm_step: float32 [4096], P(('shard', 'width')), may hold values from -0.3 to 0.3
Outputs:
- serving_query: bfloat16 [4096, 4096], P(None, 'width')
- serving_key: bfloat16 [4096, 1024], P(None, 'width')
- serving_value: bfloat16 [4096, 1024], P(None, 'width')
- column_query: float32 [4096], P('width')
- column_key: float32 [1024], P('width')
- column_value: float32 [1024], P('width')
- serve_norm: bfloat16 [4096], replicated
- whole_query: float32 [4096, 4096], P('shard', 'width')
- whole_key: float32 [4096, 1024], P('shard', 'width')
- whole_value: float32 [4096, 1024], P('shard', 'width')
All inputs are finite; a program needn't handle non-finite values. Where the computation divides by a largest or mean magnitude, that divisor is 1e-20 or more.
Results may differ from a plain program's by a relative error of at most 0.0004.
Values may be sent and summed in bfloat16 or wider, within the bound.
A program may use at most 128 MiB of HBM per device.

v0:
```python
import jax
import jax.numpy as jnp
from jax import lax
from jax.sharding import PartitionSpec as P

D_MODEL = 4096


learn_rate = 0.2
hold_rate = 0.8


def local(
    w_query,
    first_query,
    second_query,
    w_key,
    first_key,
    second_key,
    w_value,
    first_value,
    second_value,
    norm_train,
    norm_step,
):
    hold_query = hold_rate * first_query + second_query
    whole_query = w_query - learn_rate * hold_query
    hold_key = hold_rate * first_key + second_key
    whole_key = w_key - learn_rate * hold_key
    hold_value = hold_rate * first_value + second_value
    whole_value = w_value - learn_rate * hold_value
    total_query, total_key, total_value = lax.psum(
        (
            jnp.sum(jnp.abs(whole_query), axis=0),
            jnp.sum(jnp.abs(whole_key), axis=0),
            jnp.sum(jnp.abs(whole_value), axis=0),
        ),
        "shard",
    )
    column_query = total_query / D_MODEL
    column_key = total_key / D_MODEL
    column_value = total_value / D_MODEL
    narrow_query, narrow_key, narrow_value = (
        (whole_query / column_query).astype(jnp.bfloat16),
        (whole_key / column_key).astype(jnp.bfloat16),
        (whole_value / column_value).astype(jnp.bfloat16),
    )
    serving_query, serving_key, serving_value = (
        lax.all_gather(narrow_query, "shard", axis=0, tiled=True),
        lax.all_gather(narrow_key, "shard", axis=0, tiled=True),
        lax.all_gather(narrow_value, "shard", axis=0, tiled=True),
    )
    serve_norm = lax.all_gather(
        (norm_train + norm_step).astype(jnp.bfloat16), ("shard", "width"), axis=0, tiled=True
    )
    return (
        serving_query,
        serving_key,
        serving_value,
        column_query,
        column_key,
        column_value,
        serve_norm,
        whole_query,
        whole_key,
        whole_value,
    )


def solution(mesh):
    in_specs = (
        P("shard", "width"),
        P("shard", "width"),
        P("shard", "width"),
        P("shard", "width"),
        P("shard", "width"),
        P("shard", "width"),
        P("shard", "width"),
        P("shard", "width"),
        P("shard", "width"),
        P(("shard", "width")),
        P(("shard", "width")),
    )
    out_specs = (
        P(None, "width"),
        P(None, "width"),
        P(None, "width"),
        P("width"),
        P("width"),
        P("width"),
        P(),
        P("shard", "width"),
        P("shard", "width"),
        P("shard", "width"),
    )
    return jax.shard_map(local, mesh=mesh, in_specs=in_specs, out_specs=out_specs, check_vma=False)
```

profile of v0, /device:TPU:0, one launch (start us, length us, event | category | flops | bytes accessed | tf_op | source)
XLA Modules:
  0.0 276.7 jit_solution(14937335065228174620)
XLA Ops:
  7.2 0.0 all-gather.7.cloned.1.call-start
  7.2 0.0 copy-start.5
  7.2 0.0 copy-start.6
  7.3 4.0 %abs_reduce_fusion = (f32[1024]{0:T(1024)S(1)}, f32[512,1024]{1,0:T(8,128)S(1)}) fusion(f32[512,1024]{1,0:T(8,128)} %param.11, f32[512,1024]{1,0:T(8,128)} %param.13, f32[512,1024]{1,0:T(8,128)} %param.12), kind=kLoop, calls=%fused_computation.1 | loop fusion | flops 3144704 | bytes 8392704 | tf_op jit(solution)/shard_map/reduce_sum | solution.py:34
  11.3 0.0 copy-start
  11.3 0.3 abs_reduce_fusion.1
  11.6 0.0 copy-start.3
  11.6 0.0 copy-start.4
  11.6 23.4 %all-reduce = (f32[1024]{0:T(1024)S(1)}, f32[256]{0:T(256)S(1)}, f32[256]{0:T(256)S(1)}) all-reduce(f32[1024]{0:T(1024)S(1)} %get-tuple-element.17, f32[256]{0:T(256)S(1)} %get-tuple-element.19, f32[256]{0:T(256)S(1)} %get-tuple-element.13), channel_id=1, replica_groups=mesh['shard'=8,'width'=4] {'shard'}, use_global_device_ids=true, to_apply=%region_1.0 | all-reduce | flops 1536 | bytes 12288 | tf_op jit(solution)/shard_map/psum | solution.py:32
  35.0 0.0 copy-start.12
  35.0 0.7 divide_convert_fusion.2
  35.8 0.0 all-gather.7.cloned.1.call-update
  35.8 0.0 all-gather.9.cloned.1.call-start
  35.9 0.0 copy-start.13
  35.9 0.7 divide_convert_fusion.1
  36.6 0.0 all-gather.9.cloned.1.call-update
  36.6 0.0 all-gather.5.cloned.1.call-start
  36.7 0.0 copy-start.11
  36.7 0.0 copy-start.14
  36.7 0.0 copy-start.15
  36.8 1.2 divide_convert_fusion
  38.0 0.0 copy-done.4
  38.0 0.0 all-gather.5.cloned.1.call-update
  38.1 38.3 %all-gather = bf16[32,1,128]{2,1,0:T(2,128)(2,1)S(1)} all-gather(bf16[1,1,128]{2,1,0:T(2,128)(2,1)S(1)} %convert_bitcast_fusion), channel_id=1, replica_groups=mesh['shard'=8,'width'=4] {'shard','width'}, dimensions={0}, use_global_device_ids=true | all-gather | bytes 8448 | tf_op jit(solution)/shard_map/all_gather | solution.py:53
  76.3 0.6 reduce
  77.0 5.5 %all-gather.7.cloned.1.call-done = bf16[4096,256]{1,0:T(8,128)(2,1)} async-done(((bf16[512,256]{1,0:T(8,128)(2,1)}), bf16[4096,256]{1,0:T(8,128)(2,1)}) %all-gather.7.cloned.1.call-update) | async-done | bytes 2097168 | tf_op jit(solution)/shard_map/all_gather | solution.py:50
  82.5 50.4 %all-gather.9.cloned.1.call-done = bf16[4096,256]{1,0:T(8,128)(2,1)} async-done(((bf16[512,256]{1,0:T(8,128)(2,1)}), bf16[4096,256]{1,0:T(8,128)(2,1)}) %all-gather.9.cloned.1.call-update) | async-done | bytes 2097168 | tf_op jit(solution)/shard_map/all_gather | solution.py:51
  132.9 125.7 %all-gather.5.cloned.1.call-done = bf16[4096,1024]{1,0:T(8,128)(2,1)} async-done(((bf16[512,1024]{1,0:T(8,128)(2,1)}), bf16[4096,1024]{1,0:T(8,128)(2,1)}) %all-gather.5.cloned.1.call-update) | async-done | bytes 8388624 | tf_op jit(solution)/shard_map/all_gather | solution.py:49
  258.6 7.9 %copy.24 = bf16[4096,1024]{1,0:T(8,128)(2,1)} copy(bf16[4096,1024]{1,0:T(8,128)(2,1)} %all-gather.5.cloned.1.call-done) | data formatting | bytes 16777216
  266.5 1.3 copy.25
  267.8 1.0 copy-done.2
  268.9 1.3 copy.26
  (24 shorter events, 0.1 us)
Async XLA Ops:
  7.2 75.3 %all-gather.7.cloned.1.call-start = ((), (), s32[]{:S(2)}) async-start(), calls=%async_computation.1 | async-start | bytes 2359296 | tf_op jit(solution)/shard_map/all_gather | solution.py:50
  7.2 4.1 %copy-start.5 = (f32[512,256]{1,0:T(8,128)S(1)}, f32[512,256]{1,0:T(8,128)}, u32[]{:S(2)}) copy-start(f32[512,256]{1,0:T(8,128)} %param.17) | copy-start | bytes 1572868
  7.2 4.1 %copy-start.6 = (f32[512,256]{1,0:T(8,128)S(1)}, f32[512,256]{1,0:T(8,128)}, u32[]{:S(2)}) copy-start(f32[512,256]{1,0:T(8,128)} %param.19) | copy-start | bytes 1572868
  7.2 4.1 %copy-start.7 = (f32[512,256]{1,0:T(8,128)S(1)}, f32[512,256]{1,0:T(8,128)}, u32[]{:S(2)}) copy-start(f32[512,256]{1,0:T(8,128)} %param.18) | copy-start | bytes 1572868
  7.3 4.1 %copy-start.8 = (f32[512,256]{1,0:T(8,128)S(1)}, f32[512,256]{1,0:T(8,128)}, u32[]{:S(2)}) copy-start(f32[512,256]{1,0:T(8,128)} %param.14) | copy-start | bytes 1572868
  7.3 4.1 %copy-start.9 = (f32[512,256]{1,0:T(8,128)S(1)}, f32[512,256]{1,0:T(8,128)}, u32[]{:S(2)}) copy-start(f32[512,256]{1,0:T(8,128)} %param.16) | copy-start | bytes 1572868
  7.3 4.1 %copy-start.10 = (f32[512,256]{1,0:T(8,128)S(1)}, f32[512,256]{1,0:T(8,128)}, u32[]{:S(2)}) copy-start(f32[512,256]{1,0:T(8,128)} %param.15) | copy-start | bytes 1572868
  11.3 25.4 %copy-start = (f32[512,1024]{1,0:T(8,128)}, f32[512,1024]{1,0:T(8,128)S(1)}, u32[]{:S(2)}) copy-start(f32[512,1024]{1,0:T(8,128)S(1)} %get-tuple-element.38) | copy-start | bytes 6291460
  11.6 26.4 %copy-start.3 = (f32[512,256]{1,0:T(8,128)}, f32[512,256]{1,0:T(8,128)S(1)}, u32[]{:S(2)}) copy-start(f32[512,256]{1,0:T(8,128)S(1)} %get-tuple-element.40) | copy-start | bytes 1572868
  11.6 26.4 %copy-start.4 = (f32[512,256]{1,0:T(8,128)}, f32[512,256]{1,0:T(8,128)S(1)}, u32[]{:S(2)}) copy-start(f32[512,256]{1,0:T(8,128)S(1)} %get-tuple-element.39) | copy-start | bytes 1572868
  35.0 3.0 %copy-start.12 = (f32[256]{0:T(256)}, f32[256]{0:T(256)S(1)}, u32[]{:S(2)}) copy-start(f32[256]{0:T(256)S(1)} %broadcast_multiply_fusion.2) | copy-start | bytes 3076
  35.8 97.1 %all-gather.9.cloned.1.call-start = ((), (), s32[]{:S(2)}) async-start(), calls=%async_computation.2 | async-start | bytes 2359296 | tf_op jit(solution)/shard_map/all_gather | solution.py:51
  35.9 2.1 copy-start.13
  36.6 222.0 %all-gather.5.cloned.1.call-start = ((), (), s32[]{:S(2)}) async-start(), calls=%async_computation | async-start | bytes 9437184 | tf_op jit(solution)/shard_map/all_gather | solution.py:49
  36.7 1.3 copy-start.11
  36.7 1.3 copy-start.14
  36.7 1.3 copy-start.15
  258.6 7.9 %copy-start.1 = (bf16[4096,256]{1,0:T(8,128)(2,1)S(1)}, bf16[4096,256]{1,0:T(8,128)(2,1)}, u32[]{:S(2)}) copy-start(bf16[4096,256]{1,0:T(8,128)(2,1)} %all-gather.7.cloned.1.call-done) | copy-start | bytes 6291460
  266.5 2.3 copy-start.2
Sparse Core Ops, SparseCore 0:
  35.9 46.5 all-gather.6
  85.2 47.6 all-gather.8
  135.6 122.9 all-gather.4
where the time goes:
time: 277 us
  waiting for transfers between devices  182 us (66%)
  blocking collectives  61.6 us (22%)
  between operations  14 us (5%)
  local copies, waits for them, and re-layouts  11.7 us (4%)
  other arithmetic  7.63 us (3%)
    all_gather x1, waiting for transfers between devices, local(): lax.all_gather(narrow_query, 'shard', axis=0, tiled=True)  126 us
    all_gather x1, waiting for transfers between devices, local(): lax.all_gather(narrow_value, 'shard', axis=0, tiled=True)  50.4 us
    all_gather x1, blocking collectives, local(): lax.all_gather((norm_train + norm_step).astype(jnp.bfloat16), ('shard', '...  38.3 us
    psum x1, blocking collectives, local(): lax.psum((jnp.sum(jnp.abs(whole_query), axis=0), jnp.sum(jnp.abs(whole_ke...  23.4 us
    unnamed x35, local copies, waits for them, and re-layouts  11.7 us
  transfers between devices with their start and end apart: 3, of which 3 were waited for; matrix products, arithmetic and copies ran while one was open for 1% of the time, Pallas kernels for 0%

commit v1 on v0

v1 whole, which is shorter than its diff:
```python
import functools

import jax
import jax.numpy as jnp
from jax import lax
from jax.experimental import pallas as pl
from jax.experimental.pallas import tpu as pltpu
from jax.sharding import PartitionSpec as P

learn_rate = 0.2
hold_rate = 0.8
MESH = pl.DeviceIdType.MESH
TILE = 16


def gather_kernel(
    n,
    width,
    w_q,
    w_k,
    w_v,
    norm_in,
    out_q,
    out_k,
    out_v,
    col_q,
    col_k,
    col_v,
    norm_out,
    sums,
    sum_send,
    sum_recv,
    wid_send,
    wid_recv,
    nrm_send,
    nrm_recv,
    z_send,
    z_recv,
    x_send,
    x_recv,
):
    me = lax.axis_index("shard")
    me_w = lax.axis_index("width")
    depth = n // 2
    z, x = lax.div(me, 2), lax.rem(me, 2)
    rows = w_q.shape[0]
    ins, outs, cols = (w_q, w_k, w_v), (out_q, out_k, out_v), (col_q, col_k, col_v)
    extents = [ref.shape[1] for ref in ins]
    starts = [sum(extents[:i]) for i in range(3)]

    barrier = pltpu.get_barrier_semaphore()
    for k in range(1, n):
        pl.semaphore_signal(
            barrier, inc=1, device_id={"shard": lax.rem(me + k, n)}, device_id_type=MESH
        )
    for k in range(1, width):
        pl.semaphore_signal(
            barrier, inc=1, device_id={"width": lax.rem(me_w + k, width)}, device_id_type=MESH
        )

    for ref, start, extent in zip(ins, starts, extents):

        def add(i, total, ref=ref):
            for j in range(4):
                total = total + jnp.abs(ref[pl.ds(pl.multiple_of(i * 32 + j * 8, 8), 8), :])
            return total

        total = lax.fori_loop(0, rows // 32, add, jnp.zeros((8, extent), jnp.float32))
        sums[me, :, start : start + extent] = jnp.sum(total, axis=0, keepdims=True)
    norm_out[me, me_w] = norm_in[...]

    pl.semaphore_wait(barrier, n - 1 + width - 1)

    sum_copies = []
    for k in range(1, n):
        copy = pltpu.make_async_remote_copy(
            src_ref=sums.at[me],
            dst_ref=sums.at[me],
            send_sem=sum_send.at[k - 1],
            recv_sem=sum_recv.at[k - 1],
            device_id={"shard": lax.rem(me + k, n)},
            device_id_type=MESH,
        )
        copy.start()
        sum_copies.append(copy)
    wid_copies = []
    for k in range(1, width):
        copy = pltpu.make_async_remote_copy(
            src_ref=norm_in,
            dst_ref=norm_out.at[me, me_w],
            send_sem=wid_send.at[k - 1],
            recv_sem=wid_recv.at[k - 1],
            device_id={"width": lax.rem(me_w + k, width)},
            device_id_type=MESH,
        )
        copy.start()
        wid_copies.append(copy)
    for copy in sum_copies:
        copy.wait_recv()

    for ref, out, col, start, extent in zip(ins, outs, cols, starts, extents):
        total = sums[0, :, start : start + extent]
        for k in range(1, n):
            total = total + sums[k, :, start : start + extent]
        col[...] = total / (rows * n)

    for ref, out, col in zip(ins, outs, cols):
        scale = col[...]

        def narrow(i, carry, ref=ref, out=out, scale=scale):
            here = pl.multiple_of(i * TILE, TILE)
            there = pl.multiple_of(me * rows + i * TILE, TILE)
            out[pl.ds(there, TILE), :] = (ref[pl.ds(here, TILE), :] / scale).astype(jnp.bfloat16)
            return carry

        lax.fori_loop(0, rows // TILE, narrow, 0)

    part_g = TILE * max(1, round(rows * 4 / 9 / (2 * TILE)))
    part_h = rows // 2 - part_g
    g_at = (0, part_g)
    h_at = (2 * part_g, 2 * part_g + part_h)
    started = []

    def send(owner, at, size, target, send_sems, recv_sems):
        copies = []
        where = pl.ds(pl.multiple_of(owner * rows + at, TILE), size)
        for i, out in enumerate(outs):
            copy = pltpu.make_async_remote_copy(
                src_ref=out.at[where],
                dst_ref=out.at[where],
                send_sem=send_sems.at[i],
                recv_sem=recv_sems.at[i],
                device_id={"shard": target},
                device_id_type=MESH,
            )
            copy.start()
            copies.append(copy)
        started.extend(copies)
        return copies

    def arrived(copies):
        for copy in copies:
            copy.wait_recv()

    other = z * 2 + 1 - x
    step_of = (1, depth - 1)
    next_of = [lax.rem(z + step_of[d], depth) * 2 + x for d in range(2)]

    def ring_send(kind, d, s):
        at_z = lax.rem(z + s * step_of[1 - d], depth)
        column = 1 - x if kind == 2 else x
        at, size = ((g_at[d], part_g), (h_at[d], part_h), (h_at[d], part_h))[kind]
        return send(
            at_z * 2 + column,
            at,
            size,
            next_of[d],
            z_send.at[d, kind, s],
            z_recv.at[d, kind, s],
        )

    def x_own(unit):
        at, size = ((h_at[0], part_h), (h_at[1], part_h), (g_at[0], part_g), (g_at[1], part_g))[unit]
        return send(me, at, size, other, x_send.at[unit], x_recv.at[unit])

    def x_forward(d, s):
        at_z = lax.rem(z + (s + 1) * step_of[1 - d], depth)
        unit = 4 + 2 * s + d
        return send(at_z * 2 + x, g_at[d], part_g, other, x_send.at[unit], x_recv.at[unit])

    ring = {}
    crossed = [x_own(0)]
    for d in range(2):
        ring[0, d, 0] = ring_send(0, d, 0)
    crossed.append(x_own(1))
    for d in range(2):
        ring[1, d, 0] = ring_send(1, d, 0)
    crossed.append(x_own(2))
    crossed.append(x_own(3))

    for copy in wid_copies:
        copy.wait_recv()
    nrm_copies = []
    for k in range(1, n):
        copy = pltpu.make_async_remote_copy(
            src_ref=norm_out.at[me],
            dst_ref=norm_out.at[me],
            send_sem=nrm_send.at[k - 1],
            recv_sem=nrm_recv.at[k - 1],
            device_id={"shard": lax.rem(me + k, n)},
            device_id_type=MESH,
        )
        copy.start()
        nrm_copies.append(copy)

    def ring_arrival(kind, s):
        for d in range(2):
            arrived(ring[kind, d, s])
            if s + 1 < depth - 1:
                ring[kind, d, s + 1] = ring_send(kind, d, s + 1)
            if kind == 0:
                crossed.append(x_forward(d, s))

    def cross_arrival(d):
        arrived(crossed[d])
        ring[2, d, 0] = ring_send(2, d, 0)

    ring_arrival(0, 0)
    cross_arrival(0)
    ring_arrival(1, 0)
    cross_arrival(1)
    for s in range(1, depth - 1):
        ring_arrival(0, s)
        ring_arrival(2, s - 1)
        ring_arrival(1, s)
    ring_arrival(2, depth - 2)
    for copies in crossed[2:]:
        arrived(copies)
    for copy in nrm_copies:
        copy.wait_recv()
    for copy in sum_copies + wid_copies + nrm_copies + started:
        copy.wait_send()


def local(
    n,
    width,
    w_query,
    first_query,
    second_query,
    w_key,
    first_key,
    second_key,
    w_value,
    first_value,
    second_value,
    norm_train,
    norm_step,
):
    whole_query = w_query - learn_rate * (hold_rate * first_query + second_query)
    whole_key = w_key - learn_rate * (hold_rate * first_key + second_key)
    whole_value = w_value - learn_rate * (hold_rate * first_value + second_value)
    norm = (norm_train + norm_step).reshape(1, -1)
    wholes = (whole_query, whole_key, whole_value)
    rows = whole_query.shape[0]
    extents = [each.shape[1] for each in wholes]
    piece = norm.shape[1]
    depth = n // 2
    dma = pltpu.SemaphoreType.DMA
    vmem = pl.BlockSpec(memory_space=pltpu.VMEM)
    gathered = pl.pallas_call(
        functools.partial(gather_kernel, n, width),
        out_shape=[jax.ShapeDtypeStruct((rows * n, e), jnp.bfloat16) for e in extents]
        + [jax.ShapeDtypeStruct((1, e), jnp.float32) for e in extents]
        + [jax.ShapeDtypeStruct((n, width, 1, piece), jnp.float32)],
        in_specs=[vmem] * 4,
        out_specs=[vmem] * 7,
        scratch_shapes=[
            pltpu.VMEM((n, 1, sum(extents)), jnp.float32),
            dma((n - 1,)),
            dma((n - 1,)),
            dma((width - 1,)),
            dma((width - 1,)),
            dma((n - 1,)),
            dma((n - 1,)),
            dma((2, 3, depth - 1, 3)),
            dma((2, 3, depth - 1, 3)),
            dma((4 + 2 * (depth - 1), 3)),
            dma((4 + 2 * (depth - 1), 3)),
        ],
        compiler_params=pltpu.CompilerParams(
            collective_id=0, has_side_effects=True, vmem_limit_bytes=48 * 1024 * 1024
        ),
    )(*wholes, norm)
    serving_query, serving_key, serving_value, column_query, column_key, column_value, gain = gathered
    return (
        serving_query,
        serving_key,
        serving_value,
        column_query.reshape(-1),
        column_key.reshape(-1),
        column_value.reshape(-1),
        gain.reshape(-1).astype(jnp.bfloat16),
        whole_query,
        whole_key,
        whole_value,
    )


def solution(mesh):
    split = P("shard", "width")
    both = P(("shard", "width"))
    n, width = mesh.shape["shard"], mesh.shape["width"]
    return jax.shard_map(
        functools.partial(local, n, width),
        mesh=mesh,
        in_specs=(split,) * 9 + (both, both),
        out_specs=(P(None, "width"),) * 3 + (P("width"),) * 3 + (P(),) + (split,) * 3,
        check_vma=False,
    )
```

time: 277 us -> 197 us (0.71)
  waiting for transfers between devices: 182 us -> 0 us
  Pallas kernels: 0 us -> 176 us
  blocking collectives: 61.6 us -> 0 us
  between operations: 14 us -> 0.68 us
    all_gather x3 -> x0, waiting for transfers between devices: 182 us -> none  [the longest x1 126 us: local(): lax.all_gather(narrow_query, 'shard', axis=0, tiled=True)]
    pallas_call x0 -> x1, Pallas kernels: none -> 176 us  [local(): pl.pallas_call(functools.partial(gather_kernel, n, width), out_shape=[jax...]
    all_gather x1 -> x0, blocking collectives: 38.3 us -> none  [local(): lax.all_gather((norm_train + norm_step).astype(jnp.bfloat16), ('shard', '...]
    psum x1 -> x0, blocking collectives: 23.4 us -> none  [local(): lax.psum((jnp.sum(jnp.abs(whole_query), axis=0), jnp.sum(jnp.abs(whole_ke...]
    sub x0 -> x2, other arithmetic: none -> 5.64 us  [the longest x1 3.45 us: local(): w_query - learn_rate * (hold_rate * first_query + second_query)]
    reduce_sum x2 -> x0, other arithmetic: 4.24 us -> none  [the longest x1 3.99 us: local(): jnp.sum(jnp.abs(whole_query), axis=0)]
    unnamed x35 -> x14, local copies, waits for them, and re-layouts: 11.7 us -> 13.1 us
  transfers between devices with their start and end apart: 3 -> 0, of which waited for: 3 -> 0; matrix products, arithmetic and copies ran while one was open for 1% -> 0% of each run, Pallas kernels for 0% -> 0%
where the time goes in v1:
time: 197 us
  Pallas kernels  176 us (89%)
  local copies, waits for them, and re-layouts  13.1 us (7%)
  other arithmetic  6.96 us (4%)
    pallas_call x1, Pallas kernels, local(): pl.pallas_call(functools.partial(gather_kernel, n, width), out_shape=[jax...  176 us
    unnamed x14, local copies, waits for them, and re-layouts  13.1 us

profile of v1, /device:TPU:0, one launch (start us, length us, event | category | flops | bytes accessed | tf_op | source)
XLA Modules:
  0.0 196.8 jit_solution(2994617729672698503)
XLA Ops:
  0.6 0.7 add_bitcast_fusion.norm_in
  1.3 0.0 copy-start.2
  1.3 0.0 copy-start.3
  1.3 2.2 %multiply_subtract_fusion.1 = (f32[512,256]{1,0:T(8,128)S(1)}, f32[512,256]{1,0:T(8,128)S(1)}) fusion(f32[512,256]{1,0:T(8,128)} %param.17, f32[512,256]{1,0:T(8,128)} %param.19, f32[512,256]{1,0:T(8,128)} %param.18, f32[512,256]{1,0:T(8,128)} %param.14, f32[512,256]{1,0:T(8,128)} %param.16, f32[512,256]{1,0:T(8,128)} %param.15), kind=kLoop, calls=%fused_computation.1 | loop fusion | flops 1048576 | bytes 4194304 | tf_op jit(solution)/shard_map/sub | solution.py:242
  3.5 0.0 copy-start
  3.5 0.0 copy-start.1
  3.5 0.3 copy-done.2
  3.9 0.6 copy-done.3
  4.5 3.4 %multiply_subtract_fusion.w_q = f32[512,1024]{1,0:T(8,128)} fusion(f32[512,1024]{1,0:T(8,128)S(1)} %copy-done.2, f32[512,1024]{1,0:T(8,128)S(1)} %copy-done.3, f32[512,1024]{1,0:T(8,128)} %param.12), kind=kLoop, calls=%fused_computation | loop fusion | flops 2097152 | bytes 8388608 | tf_op jit(solution)/shard_map/sub | solution.py:240
  7.9 0.0 copy-done
  7.9 0.0 copy-done.1
  7.9 176.1 %shard_map.186 = (bf16[4096,1024]{1,0:T(8,128)(2,1)}, bf16[4096,256]{1,0:T(8,128)(2,1)S(1)}, bf16[4096,256]{1,0:T(8,128)(2,1)S(1)}, f32[1,1024]{1,0:T(1,128)S(1)...) custom-call(f32[512,1024]{1,0:T(8,128)} %multiply_subtract_fusion.w_q, ...), custom_call_target="tpu_custom_call" | custom-call | tf_op jit(solution)/shard_map/pallas_call | solution.py:251
  184.1 0.6 convert_reduce_fusion
  184.7 7.8 %copy.27 = bf16[4096,1024]{1,0:T(8,128)(2,1)} copy(bf16[4096,1024]{1,0:T(8,128)(2,1)} %get-tuple-element.36) | data formatting | bytes 16777216
  192.5 1.3 copy.28
  193.8 1.3 copy.29
  195.1 0.6 copy.30
  195.7 0.6 copy.31
  196.3 0.6 copy.32
Async XLA Ops:
  1.3 2.5 %copy-start.2 = (f32[512,1024]{1,0:T(8,128)S(1)}, f32[512,1024]{1,0:T(8,128)}, u32[]{:S(2)}) copy-start(f32[512,1024]{1,0:T(8,128)} %param.11) | copy-start | bytes 6291460
  1.3 3.2 %copy-start.3 = (f32[512,1024]{1,0:T(8,128)S(1)}, f32[512,1024]{1,0:T(8,128)}, u32[]{:S(2)}) copy-start(f32[512,1024]{1,0:T(8,128)} %param.13) | copy-start | bytes 6291460
  3.5 4.4 %copy-start = (f32[512,256]{1,0:T(8,128)}, f32[512,256]{1,0:T(8,128)S(1)}, u32[]{:S(2)}) copy-start(f32[512,256]{1,0:T(8,128)S(1)} %get-tuple-element.45.w_v) | copy-start | bytes 1572868
  3.5 4.4 %copy-start.1 = (f32[512,256]{1,0:T(8,128)}, f32[512,256]{1,0:T(8,128)S(1)}, u32[]{:S(2)}) copy-start(f32[512,256]{1,0:T(8,128)S(1)} %get-tuple-element.44.w_k) | copy-start | bytes 1572868
